TPU v7x, 64 devices: a 2x2x8 block of a 4x4x8 slice. The times are simulated.
64 devices in a mesh: dp: 4 (over x, y), ep: 16 (over z, core).
Axes of the slice: x: 2, y: 2, z: 8, core: 2. Of those that a mesh axis runs over, the one named last changes fastest.
The devices are a block of a 4x4x8 slice.
Arguments:
- x_tokens: bfloat16 [4096, 1536], P(('dp', 'ep')), parts along dimension 0
- slot_expert: int32 [320], replicated
- w1_slots: bfloat16 [320, 1536, 512], P('ep')
- w3_slots: bfloat16 [320, 1536, 512], P('ep')
- w2_slots: bfloat16 [320, 512, 1536], P('ep')
- assign: int32 [4096, 6], P(('dp', 'ep')), parts along dimension 0
- w_router: bfloat16 [1536, 64], replicated
- w1_shared: bfloat16 [1536, 1024], replicated
- w3_shared: bfloat16 [1536, 1024], replicated
- w2_shared: bfloat16 [1024, 1536], replicated
Outputs:
- output: bfloat16 [4096, 1536], P(('dp', 'ep')), parts along dimension 0
There are 4 independent parts. A program takes and returns all parts, laid end to end along the dimension named above; an argument that names none is the same for every part.
All inputs are finite; a program needn't handle non-finite values.
Results may differ from a plain program's by a relative error of at most 0.00102.
Values are sent between devices in bfloat16 or wider.
A program may use at most 768 MiB of HBM per device.

v0:
```python
import jax
import jax.numpy as jnp
from jax import lax
from jax.sharding import PartitionSpec as P

ROUTE_SCALE = 2.5


def gate_weights(x_tokens, assign, slot_expert, w_router):
    logits = jnp.dot(x_tokens, w_router, preferred_element_type=jnp.float32)
    gate_prob = jax.nn.sigmoid(logits)
    is_kept = assign >= 0
    chosen = jnp.take(slot_expert, jnp.maximum(assign, 0))
    picked = jnp.where(is_kept, jnp.take_along_axis(gate_prob, chosen, axis=1), 0.0)
    gate_total = jnp.sum(picked, axis=1, keepdims=True)
    return ROUTE_SCALE * picked / jnp.maximum(gate_total, 1e-30), is_kept


def shared_expert(x_tokens, w1_shared, w3_shared, w2_shared):
    h_gate = jnp.dot(x_tokens, w1_shared, preferred_element_type=jnp.float32)
    h_up = jnp.dot(x_tokens, w3_shared, preferred_element_type=jnp.float32)
    mid_act = (jax.nn.silu(h_gate) * h_up).astype(jnp.bfloat16)
    return jnp.dot(mid_act, w2_shared, preferred_element_type=jnp.float32)


def solution(mesh):
    group_size = mesh.shape['ep']

    def device_step(x_tokens, slot_expert, w1_slots, w3_slots, w2_slots, assign, w_router, w1_shared, w3_shared, w2_shared):
        tok_dev, dim_model = x_tokens.shape
        top_k = assign.shape[1]
        local_slots = w1_slots.shape[0]
        num_slots = local_slots * group_size
        cap_rows = max(4, (3 * tok_dev * top_k) // num_slots)
        route_weight, is_kept = gate_weights(x_tokens, assign, slot_expert, w_router)
        shared_out = shared_expert(x_tokens, w1_shared, w3_shared, w2_shared)
        flat_slot = jnp.where(is_kept, assign, num_slots).reshape(-1)
        onehot = (flat_slot[:, None] == jnp.arange(num_slots, dtype=jnp.int32)[None, :]).astype(jnp.int32)
        slot_rank = jnp.sum(jnp.cumsum(onehot, axis=0) * onehot, axis=1) - 1
        dummy_row = num_slots * cap_rows
        row_pos = jnp.where(flat_slot < num_slots, flat_slot * cap_rows + slot_rank, dummy_row)
        token_ids = jnp.arange(tok_dev * top_k, dtype=jnp.int32) // top_k
        row_token = jnp.full((dummy_row + 1,), tok_dev, jnp.int32).at[row_pos].set(token_ids)[:dummy_row]
        send_rows = jnp.take(x_tokens, row_token, axis=0, mode='fill', fill_value=0)
        recv_rows = lax.all_to_all(send_rows, 'ep', 0, 0, tiled=True)
        recv_rows = recv_rows.reshape(group_size, local_slots, cap_rows, dim_model)
        h_gate = jnp.einsum('jlcd,ldf->jlcf', recv_rows, w1_slots, preferred_element_type=jnp.float32)
        h_up = jnp.einsum('jlcd,ldf->jlcf', recv_rows, w3_slots, preferred_element_type=jnp.float32)
        mid_act = (jax.nn.silu(h_gate) * h_up).astype(jnp.bfloat16)
        expert_out = jnp.einsum('jlcf,lfd->jlcd', mid_act, w2_slots, preferred_element_type=jnp.float32).astype(jnp.bfloat16)
        back_rows = lax.all_to_all(expert_out.reshape(dummy_row, dim_model), 'ep', 0, 0, tiled=True)
        gathered = jnp.take(back_rows, jnp.minimum(row_pos, dummy_row - 1), axis=0).reshape(tok_dev, top_k, dim_model)
        routed = jnp.sum(route_weight[:, :, None] * gathered, axis=1)
        return (shared_out + routed).astype(jnp.bfloat16)

    token_spec = P(('dp', 'ep'), None)
    slot_spec = P('ep', None, None)
    return jax.shard_map(device_step, mesh=mesh, in_specs=(token_spec, P(), slot_spec, slot_spec, slot_spec, token_spec, P(), P(), P(), P()), out_specs=token_spec, check_vma=False)
```

profile of v0, /device:TPU:21, one launch (start us, length us, event | category | flops | bytes accessed | tf_op | source)
XLA Modules:
  0.0 281.3 jit_solution(15135712117434354315)
XLA Ops:
  0.0 0.0 copy-start
  0.0 0.0 copy-start.2
  0.0 0.9 copy.23
  0.9 0.1 eq.26
  1.1 0.1 reshape.149
  1.2 0.1 copy.26
  1.4 0.2 fusion.23
  1.6 0.0 copy-start.3
  1.6 0.9 copy-done.3
  2.5 1.3 broadcast_add_fusion
  3.8 0.2 fusion.25
  4.1 0.1 sub.15
  4.2 0.1 lt.84
  4.4 0.1 mul.62
  4.6 2.9 %scatter_custom_fusion = s32[1281]{0:T(1024)S(1)} fusion(s32[384]{0:T(512)S(1)} %get-tuple-element.6, s32[384]{0:T(512)S(1)} %add_select_fusion, s32[]{:T(128)} %constant.63.clone.1), kind=kCustom, calls=%fused_computation.66 | custom fusion | bytes 5128 | tf_op jit(solution)/shard_map/scatter | solution.py:43
  7.5 0.1 slice.14
  7.6 0.0 copy-done.2
  7.6 5.4 %gather_fusion.1 = bf16[1280,1536]{1,0:T(8,128)(2,1)} fusion(bf16[64,1536]{1,0:T(8,128)(2,1)S(1)} %copy-done.2, s32[2048]{0:T(1024)S(1)} %pad_clamp_fusion), kind=kCustom, calls=%fused_computation.1 | custom fusion | bytes 7869440 | tf_op jit(solution)/shard_map/jit(_take)/gather | solution.py:44
  13.1 2.5 broadcast_select_fusion
  15.5 100.8 %all_to_all.18 = bf16[16,80,1536]{2,1,0:T(8,128)(2,1)S(1)} all-to-all(bf16[16,80,1536]{2,1,0:T(8,128)(2,1)S(1)} %broadcast_select_fusion), channel_id=1, replica_groups=mesh['dp'=4,'ep'=16] {'ep'}, dimensions={0} | all-to-all | bytes 7864320 | tf_op jit(solution)/shard_map/all_to_all | solution.py:45
  116.3 4.1 %copy.28 = bf16[16,80,1536]{2,0,1:T(8,128)(2,1)} copy(bf16[16,80,1536]{2,1,0:T(8,128)(2,1)S(1)} %all_to_all.18) | data formatting | bytes 7864320 | tf_op jit(solution)/shard_map/all_to_all | solution.py:45
  120.4 18.2 %fusion.2 = f32[20,16,4,512]{3,1,2,0:T(8,128)} fusion(bf16[16,20,4,1536]{3,0,2,1:T(8,128)(2,1)} %bitcast.70, bf16[20,1536,512]{2,1,0:T(8,128)(2,1)} %param.13), kind=kOutput, calls=%fused_computation.7 | convolution fusion | flops 2013265920 | bytes 38010880 | tf_op jit(solution)/shard_map/jlcd,ldf->jlcf/dot_general | solution.py:48
  138.6 27.0 %fusion.6 = bf16[20,16,4,1536]{3,1,2,0:T(8,128)(2,1)} fusion(bf16[20,512,1536]{2,1,0:T(8,128)(2,1)} %param.14, f32[20,16,4,512]{3,1,2,0:T(8,128)} %fusion.2, bf16[16,20,4,1536]{3,0,2,1:T(8,128)(2,1)} %bitcast.71, bf16[20,1536,512]{2,1,0:T(8,128)(2,1)} %param.12), kind=kOutput, calls=%fused_computation.11 | convolution fusion | flops 4032430080 | bytes 73400320 | tf_op jit(solution)/shard_map/jlcf,lfd->jlcd/dot_general | solution.py:50
  165.6 6.2 %copy.29 = bf16[16,80,1536]{2,1,0:T(8,128)(2,1)} copy(bf16[16,80,1536]{2,0,1:T(8,128)(2,1)} %bitcast.72) | data formatting | bytes 7864320 | tf_op jit(solution)/shard_map/all_to_all | solution.py:51
  171.8 0.0 copy-start.1
  171.8 5.0 %all-to-all-start.1 = ((bf16[16,80,1536]{2,1,0:T(8,128)(2,1)}), bf16[16,80,1536]{2,1,0:T(8,128)(2,1)}, u32[]{:S(2)}, u32[]{:S(2)}) async-start(bf16[16,80,1536]{2,1,0:T(8,128)(2,1)} %copy.29), calls=%async_computation.1 | async-start | bytes 7864320 | tf_op jit(solution)/shard_map/all_to_all | solution.py:51
  176.7 0.1 reshape.154
  176.9 0.0 copy-done.1
  176.9 2.8 gather_fusion
  179.7 0.1 reshape.153
  179.9 0.1 reshape.176
  180.0 1.1 fusion.22
  181.2 2.9 %gather_fusion.3 = f32[384]{0:T(512)S(1)} fusion(f32[64,64]{1,0:T(8,128)S(1)} %fusion.22, s32[384]{0:T(512)S(1)} %reshape.176), kind=kCustom, calls=%fused_computation.3 | custom fusion | bytes 6144 | tf_op jit(solution)/shard_map/jit(take_along_axis)/gather | solution.py:14
  184.0 0.1 reshape.179
  184.2 0.1 fusion.42
  184.3 0.1 multiply_divide_fusion
  184.4 3.3 %fusion.44 = f32[64,1024]{1,0:T(8,128)} fusion(bf16[64,1536]{1,0:T(8,128)(2,1)S(1)} %copy-done.2, bf16[1536,1024]{1,0:T(8,128)(2,1)} %param.17), kind=kOutput, calls=%fused_computation.81 | convolution fusion | flops 201326592 | bytes 3604480 | tf_op jit(solution)/shard_map/dot_general | solution.py:20
  187.7 76.1 %all-to-all-done.1 = bf16[16,80,1536]{2,1,0:T(8,128)(2,1)} async-done(((bf16[16,80,1536]{2,1,0:T(8,128)(2,1)}), bf16[16,80,1536]{2,1,0:T(8,128)(2,1)}, u32[]{:S(2)}, u32[]{:S(2)}) %all-to-all-start.1) | async-done | bytes 3932192 | tf_op jit(solution)/shard_map/all_to_all | solution.py:51
  263.7 6.9 %gather_fusion.2 = bf16[384,1536]{1,0:T(8,128)(2,1)} fusion(bf16[1280,1536]{1,0:T(8,128)(2,1)} %bitcast.16, s32[1024]{0:T(1024)S(1)} %pad_clamp_fusion.1), kind=kCustom, calls=%fused_computation.2 | custom fusion | bytes 2360832 | tf_op jit(solution)/shard_map/jit(_take)/gather | solution.py:52
  270.6 3.1 %gather.25 = bf16[64,6,1536]{2,1,0:T(8,128)(2,1)} reshape(bf16[384,1536]{1,0:T(8,128)(2,1)} %gather_fusion.2) | data formatting | bytes 2359296 | tf_op jit(solution)/shard_map/jit(_take)/gather | solution.py:52
  273.7 3.6 %multiply_reduce_fusion = f32[64,1536]{1,0:T(8,128)} fusion(bf16[64,6,1536]{2,1,0:T(8,128)(2,1)} %gather.25, f32[64,6]{1,0:T(8,128)S(1)} %multiply_divide_fusion, pred[64,6]{1,0:T(8,128)(4,1)S(1)} %get-tuple-element.9), kind=kLoop, calls=%fused_computation.13 | loop fusion | flops 2260992 | bytes 1574784 | tf_op jit(solution)/shard_map/reduce_sum | solution.py:53
  277.3 0.0 copy-done
  277.3 3.9 %fusion.13 = bf16[64,1536]{1,0:T(8,128)(2,1)} fusion(f32[64,1536]{1,0:T(8,128)} %multiply_reduce_fusion, bf16[1024,1536]{1,0:T(8,128)(2,1)S(1)} %copy-done, bf16[64,1536]{1,0:T(8,128)(2,1)S(1)} %copy-done.2, bf16[1536,1024]{1,0:T(8,128)(2,1)} %param.18, f32[64,1024]{1,0:T(8,128)} %fusion.44), kind=kOutput, calls=%fused_computation.22 | convolution fusion | flops 403243008 | bytes 7340032 | tf_op jit(solution)/shard_map/dot_general | solution.py:23
  (15 shorter events, 0.2 us)
Async XLA Ops:
  0.0 277.3 %copy-start = (bf16[1024,1536]{1,0:T(8,128)(2,1)S(1)}, bf16[1024,1536]{1,0:T(8,128)(2,1)}, u32[]{:S(2)}) copy-start(bf16[1024,1536]{1,0:T(8,128)(2,1)} %param.19) | copy-start | bytes 9437188
  0.0 7.6 %copy-start.2 = (bf16[64,1536]{1,0:T(8,128)(2,1)S(1)}, bf16[64,1536]{1,0:T(8,128)(2,1)}, u32[]{:S(2)}) copy-start(bf16[64,1536]{1,0:T(8,128)(2,1)} %param.10) | copy-start | bytes 589828
  1.6 0.9 copy-start.3
  171.8 5.1 %copy-start.1 = (s32[320]{0:T(512)S(1)}, s32[320]{0:T(512)}, u32[]{:S(2)}) copy-start(s32[320]{0:T(512)} %param.11) | copy-start | bytes 3844
  171.8 92.0 %all-to-all-start.1 = ((bf16[16,80,1536]{2,1,0:T(8,128)(2,1)}), bf16[16,80,1536]{2,1,0:T(8,128)(2,1)}, u32[]{:S(2)}, u32[]{:S(2)}) async-start(bf16[16,80,1536]{2,1,0:T(8,128)(2,1)} %copy.29), calls=%async_computation.1 | async-start | bytes 7864320 | tf_op jit(solution)/shard_map/all_to_all | solution.py:51
where the time goes:
time: 282 us; the launch traced here: 281 us
  blocking collectives  101 us (36%)
  waiting for transfers between devices  76.1 us (27%)
  matrix products  53.5 us (19%)
  local copies, waits for them, and re-layouts  37.5 us (13%)
  other arithmetic  8.2 us (3%)
  starting transfers between devices  4.98 us (2%)
    all_to_all x1, blocking collectives, device_step(): recv_rows = lax.all_to_all(send_rows, 'ep', 0, 0, tiled=True)  101 us
    all_to_all x1, waiting for transfers between devices, device_step(): lax.all_to_all(expert_out.reshape(dummy_row, dim_model), 'ep', 0, 0, tile...  76.1 us
    dot_general x1, matrix products, device_step(): jnp.einsum('jlcf,lfd->jlcd', mid_act, w2_slots, preferred_element_type=jn...  27 us
    dot_general x1, matrix products, device_step(): jnp.einsum('jlcd,ldf->jlcf', recv_rows, w3_slots, preferred_element_type=...  18.2 us
    gather x2, local copies, waits for them, and re-layouts, device_step(): jnp.take(back_rows, jnp.minimum(row_pos, dummy_row - 1), axis=0)  9.95 us
    all_to_all x1, local copies, waits for them, and re-layouts, device_step(): lax.all_to_all(expert_out.reshape(dummy_row, dim_model), 'ep', 0, 0, tile...  6.16 us
  transfers between devices with their start and end apart: 1, of which 1 were waited for; matrix products, arithmetic and copies ran while one was open for 4% of the time, Pallas kernels for 0%

commit v1 on v0

v1 whole, which is shorter than its diff:
```python
import functools

import jax
import jax.numpy as jnp
from jax import lax
from jax.experimental import pallas as pl
from jax.experimental.pallas import tpu as pltpu
from jax.sharding import PartitionSpec as P

ROUTE_SCALE = 2.5
MESH = pl.DeviceIdType.MESH
F32 = jnp.float32
BF16 = jnp.bfloat16
RING = 9
QUOTA = {0: 12}
QUOTA_FAR = 4
CAPS = {0: 144, 1: 48, 2: 32, 3: 16, 4: 16}
FIT_STEPS = 8


def gate_weights(x_tokens, assign, slot_expert, w_router):
    logits = jnp.dot(x_tokens, w_router, preferred_element_type=jnp.float32)
    gate_prob = jax.nn.sigmoid(logits)
    is_kept = assign >= 0
    chosen = jnp.take(slot_expert, jnp.maximum(assign, 0))
    picked = jnp.where(is_kept, jnp.take_along_axis(gate_prob, chosen, axis=1), 0.0)
    gate_total = jnp.sum(picked, axis=1, keepdims=True)
    return ROUTE_SCALE * picked / jnp.maximum(gate_total, 1e-30), is_kept


def shared_expert(x_tokens, w1_shared, w3_shared, w2_shared):
    h_gate = jnp.dot(x_tokens, w1_shared, preferred_element_type=jnp.float32)
    h_up = jnp.dot(x_tokens, w3_shared, preferred_element_type=jnp.float32)
    mid_act = (jax.nn.silu(h_gate) * h_up).astype(jnp.bfloat16)
    return jnp.dot(mid_act, w2_shared, preferred_element_type=jnp.float32)


def plain_step(group_size, x_tokens, slot_expert, w1_slots, w3_slots, w2_slots, assign, w_router, w1_shared, w3_shared, w2_shared):
    tok_dev, dim_model = x_tokens.shape
    top_k = assign.shape[1]
    local_slots = w1_slots.shape[0]
    num_slots = local_slots * group_size
    cap_rows = max(4, (3 * tok_dev * top_k) // num_slots)
    route_weight, is_kept = gate_weights(x_tokens, assign, slot_expert, w_router)
    shared_out = shared_expert(x_tokens, w1_shared, w3_shared, w2_shared)
    flat_slot = jnp.where(is_kept, assign, num_slots).reshape(-1)
    onehot = (flat_slot[:, None] == jnp.arange(num_slots, dtype=jnp.int32)[None, :]).astype(jnp.int32)
    slot_rank = jnp.sum(jnp.cumsum(onehot, axis=0) * onehot, axis=1) - 1
    dummy_row = num_slots * cap_rows
    row_pos = jnp.where(flat_slot < num_slots, flat_slot * cap_rows + slot_rank, dummy_row)
    token_ids = jnp.arange(tok_dev * top_k, dtype=jnp.int32) // top_k
    row_token = jnp.full((dummy_row + 1,), tok_dev, jnp.int32).at[row_pos].set(token_ids)[:dummy_row]
    send_rows = jnp.take(x_tokens, row_token, axis=0, mode='fill', fill_value=0)
    recv_rows = lax.all_to_all(send_rows, 'ep', 0, 0, tiled=True)
    recv_rows = recv_rows.reshape(group_size, local_slots, cap_rows, dim_model)
    h_gate = jnp.einsum('jlcd,ldf->jlcf', recv_rows, w1_slots, preferred_element_type=jnp.float32)
    h_up = jnp.einsum('jlcd,ldf->jlcf', recv_rows, w3_slots, preferred_element_type=jnp.float32)
    mid_act = (jax.nn.silu(h_gate) * h_up).astype(jnp.bfloat16)
    expert_out = jnp.einsum('jlcf,lfd->jlcd', mid_act, w2_slots, preferred_element_type=jnp.float32).astype(jnp.bfloat16)
    back_rows = lax.all_to_all(expert_out.reshape(dummy_row, dim_model), 'ep', 0, 0, tiled=True)
    gathered = jnp.take(back_rows, jnp.minimum(row_pos, dummy_row - 1), axis=0).reshape(tok_dev, top_k, dim_model)
    routed = jnp.sum(route_weight[:, :, None] * gathered, axis=1)
    return (shared_out + routed).astype(jnp.bfloat16)


class Plan:
    def __init__(self, n, tok, top_k, slots):
        self.n, self.nz, self.tok, self.top_k, self.slots = n, n // 2, tok, top_k, slots
        nz = self.nz
        order = [0]
        for d in range(1, nz // 2):
            order += [d, nz - d]
        order.append(nz // 2)
        self.order = order
        self.blocks = [(d, f) for d in order for f in (0, 1)]
        self.pos = {b: i for i, b in enumerate(self.blocks)}
        self.ad = lambda d: min(d, nz - d)
        self.quota = [QUOTA.get(self.ad(d), QUOTA_FAR) for d, _ in self.blocks]
        self.cap = [CAPS[self.ad(d)] for d, _ in self.blocks]
        self.off = [sum(self.cap[:i]) for i in range(n)]
        self.rows = sum(self.cap)
        self.groups = n // 4
        self.grp_rows = [sum(self.quota[4 * g:4 * g + 4]) for g in range(self.groups)]
        self.grp_off = [sum(self.grp_rows[:g]) for g in range(self.groups)]
        self.m = sum(self.grp_rows)
        self.neg = [self.pos[((nz - d) % nz, f)] for d, f in self.blocks]


def iota(shape, dim):
    return lax.broadcasted_iota(jnp.int32, shape, dim)


def onehot(mask):
    return jnp.where(mask, 1.0, 0.0).astype(BF16)


def dot(a, b):
    return jnp.dot(a, b, preferred_element_type=F32)


def dot_nt(a, b):
    return lax.dot_general(a, b, (((1,), (1,)), ((), ())), preferred_element_type=F32)


def divmod_const(v, d):
    q = ((v.astype(F32) + 0.5) * (1.0 / d)).astype(jnp.int32)
    return q, v - q * d


def step_kernel(plan, n_dp, x_ref, assign_ref, se_row_ref, se_col_ref, wr_ref, w1_hbm, w3_hbm, w2_hbm, s1_hbm, s3_hbm, s2_hbm,
                y_ref, flag_ref, x_all, xo, ret, back, z_ref, meta, meta_all, flags, w1b, w3b, w2b,
                wsem, ring_s, ring_r, d2d_s, d2d_r, meta_s, meta_r, flag_s, flag_r, ret_s, ret_r):
    n, nz, tok, top_k, slots = plan.n, plan.nz, plan.tok, plan.top_k, plan.slots
    half = tok // 2
    dim = x_ref.shape[1]
    ff = w1b.shape[2]
    n_shared = s1_hbm.shape[1] // ff
    total = slots + n_shared
    me = lax.axis_index('ep')
    my_dp = lax.axis_index('dp')
    z, c = me // 2, lax.rem(me, 2)

    def dev_of(d, f):
        zz = lax.rem(z + d, nz)
        cc = c if f == 0 else 1 - c
        return zz * 2 + cc

    def peer(d, f):
        return {'dp': my_dp, 'ep': dev_of(d, f)}

    def weight_copies(v):
        b = v % RING
        if v < n_shared:
            cols = pl.ds(v * ff, ff)
            return [pltpu.make_async_copy(s1_hbm.at[:, cols], w1b.at[b], wsem.at[b, 0]),
                    pltpu.make_async_copy(s3_hbm.at[:, cols], w3b.at[b], wsem.at[b, 1]),
                    pltpu.make_async_copy(s2_hbm.at[cols, :], w2b.at[b], wsem.at[b, 2])]
        return slot_copies(v - n_shared, b)

    def slot_copies(s, b):
        return [pltpu.make_async_copy(w1_hbm.at[s], w1b.at[b], wsem.at[b, 0]),
                pltpu.make_async_copy(w3_hbm.at[s], w3b.at[b], wsem.at[b, 1]),
                pltpu.make_async_copy(w2_hbm.at[s], w2b.at[b], wsem.at[b, 2])]

    for v in range(RING):
        for cp in weight_copies(v):
            cp.start()

    barrier = pltpu.get_barrier_semaphore()
    for d, f in plan.blocks[1:]:
        pl.semaphore_signal(barrier, inc=1, device_id=peer(d, f), device_id_type=MESH)
    for g in range(1, n_dp):
        pl.semaphore_signal(barrier, inc=1, device_id={'dp': lax.rem(my_dp + g, n_dp), 'ep': me}, device_id_type=MESH)
    pl.semaphore_wait(barrier, n - 1 + n_dp - 1)

    def hcp(src, d, f, h, ss, rs, to):
        return pltpu.make_async_remote_copy(
            src_ref=src.at[pl.ds(h * half, half)], dst_ref=x_all.at[plan.pos[(d, f)], pl.ds(h * half, half)],
            send_sem=ss.at[d, h], recv_sem=rs.at[d, h], device_id=to, device_id_type=MESH)

    sib = peer(0, 1)
    right, left = peer(1, 0), peer(nz - 1, 0)
    mid = nz // 2
    sends = []

    def start(cp):
        cp.start()
        sends.append(cp)

    def from_left(hop):
        return nz - hop

    def ring_in(d):
        return x_all.at[plan.pos[(d, 0)]]

    def wait_in(d, f, h, ss, rs):
        hcp(x_ref, d, f, h, ss, rs, sib).wait_recv()

    for h in range(2):
        start(hcp(x_ref, from_left(1), 0, h, ring_s, ring_r, right))
        start(hcp(x_ref, 1, 0, h, ring_s, ring_r, left))
    for h in range(2):
        start(hcp(x_ref, 0, 1, h, d2d_s, d2d_r, sib))

    def ring_step(hop):
        for h in range(2):
            d = from_left(hop - 1)
            wait_in(d, 0, h, ring_s, ring_r)
            if hop < mid or h == 0:
                start(hcp(ring_in(d), from_left(hop), 0, h, ring_s, ring_r, right))
            start(hcp(ring_in(d), d, 1, h, d2d_s, d2d_r, sib))
            d = hop - 1
            wait_in(d, 0, h, ring_s, ring_r)
            if hop < mid or h == 1:
                start(hcp(ring_in(d), hop, 0, h, ring_s, ring_r, left))
            start(hcp(ring_in(d), d, 1, h, d2d_s, d2d_r, sib))

    nc = tok * top_k
    sp = se_row_ref.shape[1]
    x_own = x_ref[...]
    x_all[plan.pos[(0, 0)]] = x_own
    logits = dot(x_own, wr_ref[...])
    gate = jax.nn.sigmoid(logits)
    n_exp = gate.shape[1]
    assign = assign_ref[...]
    a_col = jnp.concatenate([assign[:, k:k + 1] for k in range(top_k)], axis=0)
    se_row = se_row_ref[...]
    se_col = se_col_ref[...]

    def slot_geometry(ids):
        dev, loc = divmod_const(ids, slots)
        dz = (dev >> 1) - z
        dz = jnp.where(dz < 0, dz + nz, dz)
        fl = (dev & 1) ^ c
        ad = jnp.minimum(dz, nz - dz)
        near = jnp.where(ad == 0, fl, ad + 1)
        key = (near * 512 + ((ids * 111 + me * 101) & 511)) * 512 + ids
        return dev, loc, dz, fl, ad, key

    id_row, id_col = iota((1, sp), 1), iota((sp, 1), 0)
    dev_r, loc_r, dz_r, fl_r, ad_r, key_r = slot_geometry(id_row)
    dev_c, _, _, _, _, key_c = slot_geometry(id_col)

    def by_ad(table, default):
        v = jnp.full((1, sp), default, F32)
        for a, t in table.items():
            v = jnp.where(ad_r == a, float(t), v)
        return v

    quota_r = by_ad(QUOTA, float(QUOTA_FAR))
    cap_r = by_ad(CAPS, 0.0)
    off_r = jnp.zeros((1, sp), F32)
    for i, (d, f) in enumerate(plan.blocks):
        off_r = jnp.where((dz_r == d) & (fl_r == f), float(plan.off[i] // 8), off_r)

    same = se_col == se_row
    same_m = onehot(same)
    near_m = onehot(same & (key_c < key_r))
    less_m = onehot((dev_c == dev_r) & (id_col < id_row))
    pick_s = onehot(a_col == id_row)
    rep = lambda v: jnp.broadcast_to(v, (8, sp))
    given = rep(jnp.sum(pick_s.astype(F32), axis=0, keepdims=True))
    n_r = dot(given.astype(BF16), same_m)
    e_c = dot_nt(pick_s, rep(se_row.astype(F32)).astype(BF16))[:, 0:1].astype(jnp.int32)
    kept_c = a_col >= 0
    e_c = jnp.where(kept_c, e_c, -1)
    hot_e = jnp.where(e_c == iota((nc, n_exp), 1), 1.0, 0.0)
    before = onehot(iota((nc, nc), 1) < iota((nc, nc), 0))
    r_c = jnp.sum(dot(before, hot_e.astype(BF16)) * hot_e, axis=1, keepdims=True)

    ring_step(2)

    lim = rep(quota_r)
    quota8, cap8 = lim, rep(cap_r)
    for _ in range(FIT_STEPS):
        cq = dot(lim.astype(BF16), near_m)
        cnt = jnp.clip(n_r - cq, 0.0, lim)
        base = dot(cnt.astype(BF16), less_m)
        lim = jnp.minimum(lim, jnp.maximum(cap8 - base, 0.0))
    cq = dot(lim.astype(BF16), near_m)
    cnt = jnp.clip(n_r - cq, 0.0, lim)
    base = dot(cnt.astype(BF16), less_m)
    over = jnp.max(jnp.where((cnt > 0.0) & (base + cnt > cap8), 1.0, 0.0))

    ring_step(3)

    cq1, lim1, base1 = cq[0:1], lim[0:1], base[0:1]
    sel = (e_c == se_row) & (r_c >= cq1) & (r_c < cq1 + lim1) & kept_c
    rows = [loc_r.astype(F32), dev_r.astype(F32), jnp.minimum(cq1, 128.0), jnp.minimum(base1, 256.0), off_r, jnp.ones((1, sp), F32)]
    row_i = iota((8, sp), 0)
    table = jnp.zeros((8, sp), F32)
    for i, r in enumerate(rows):
        table = jnp.where(row_i == i, r, table)
    val = dot_nt(onehot(sel), table.astype(BF16))
    loc_v, dev_v, cq_v, base_v, off_v, ok_v = [val[:, i:i + 1] for i in range(6)]
    placed = ok_v > 0.5
    r_in = r_c - cq_v
    code = jnp.where(placed, dev_v * 512.0 + loc_v * 16.0 + r_in, -1.0)
    q_c = jnp.where(placed, off_v * 8.0 + base_v + r_in, -1.0).astype(jnp.int32)
    lost = jnp.max(jnp.where(kept_c & jnp.logical_not(placed), 1.0, 0.0))
    my_flag = jnp.maximum(over, lost)

    lane = iota((tok, 128), 1)
    packed = jnp.full((tok, 128), -1.0, F32)
    for k in range(top_k):
        packed = jnp.where(lane == k, code[k * tok:(k + 1) * tok], packed)
    packed_t = jnp.transpose(packed)[0:8, :]
    meta[:, 0:tok] = jnp.where(iota((8, tok), 0) == 7, my_flag, packed_t)
    meta[:, tok:] = jnp.zeros((8, 128 - tok), F32)
    meta_all[0] = meta[...]

    picked = []
    for k in range(top_k):
        hot = hot_e[k * tok:(k + 1) * tok]
        picked.append(jnp.sum(hot * gate, axis=1, keepdims=True))
    gate_total = picked[0]
    for v in picked[1:]:
        gate_total = gate_total + v
    weight = [ROUTE_SCALE * v / jnp.maximum(gate_total, 1e-30) for v in picked]

    def meta_copy(i):
        d, f = plan.blocks[i]
        return pltpu.make_async_remote_copy(
            src_ref=meta, dst_ref=meta_all.at[plan.neg[i]], send_sem=meta_s.at[i], recv_sem=meta_r.at[plan.neg[i]],
            device_id=peer(d, f), device_id_type=MESH)

    for i in range(1, n):
        meta_copy(i).start()

    def wait_weights(b):
        for cp in slot_copies(0, b):
            cp.wait()

    def act(rows_, b):
        h1 = dot(rows_, w1b[b])
        h3 = dot(rows_, w3b[b])
        return (jax.nn.silu(h1) * h3).astype(BF16)

    for v in range(n_shared):
        for cp in weight_copies(v):
            cp.wait()
        part = dot(act(x_own, v), w2b[v])
        if v == 0:
            z_ref[...] = part
        else:
            z_ref[...] += part
        for cp in weight_copies(v + RING):
            cp.start()

    ring_step(4)
    for h in range(2):
        wait_in(mid, 0, h, ring_s, ring_r)
        start(hcp(ring_in(mid), mid, 1, h, d2d_s, d2d_r, sib))

    for i in range(1, n):
        meta_copy(plan.neg[i]).wait_recv()
    codes = [meta_all[i] for i in range(n)]
    grp_flag = codes[0]
    for i in range(1, n):
        grp_flag = jnp.maximum(grp_flag, codes[i])
    grp_flag = jnp.where(iota((8, 128), 0) == 7, grp_flag, 0.0)
    flags[0] = grp_flag

    def flag_copy(g):
        return pltpu.make_async_remote_copy(
            src_ref=flags.at[0], dst_ref=flags.at[g], send_sem=flag_s.at[g], recv_sem=flag_r.at[g],
            device_id={'dp': lax.rem(my_dp + g, n_dp), 'ep': me}, device_id_type=MESH)

    for d in plan.order:
        for h in range(2):
            wait_in(d, 1, h, d2d_s, d2d_r)

    sels = []
    for g in range(plan.groups):
        mg = plan.grp_rows[g]
        rr = iota((slots * mg, 1), 0)
        loc, w = divmod_const(rr, mg)
        parts = []
        lo = 0
        src_of = jnp.zeros((slots * mg, 1), jnp.int32)
        for i4 in range(4):
            i = 4 * g + i4
            inside = (w >= lo) & (w < lo + plan.quota[i])
            row_code = jnp.where(inside, loc * 16 + (w - lo), -7)
            src_of = jnp.where(inside, i4, src_of)
            cd = codes[i].astype(jnp.int32) - me * 512
            hit = jnp.zeros((slots * mg, tok), F32)
            for k in range(top_k):
                hit = jnp.where(row_code == cd[k:k + 1, 0:tok], 1.0, hit)
            parts.append(hit)
            lo += plan.quota[i]
        sel_g = jnp.concatenate(parts, axis=1).astype(BF16)
        xs = dot(sel_g, x_all[4 * g:4 * g + 4].reshape(4 * tok, dim))
        xo[:, plan.grp_off[g]:plan.grp_off[g] + mg, :] = xs.astype(BF16).reshape(slots, mg, dim)
        used = dot_nt(jnp.ones((8, 4 * tok), BF16), sel_g)
        sels.append(used)

    for g in range(1, n_dp):
        flag_copy(g).start()

    def slot_step(s, carry):
        v = s + n_shared
        b = lax.rem(v, RING)
        wait_weights(b)
        xo[s] = dot(act(xo[s], b), w2b[b]).astype(BF16)

        @pl.when(v + RING < total)
        def _():
            for cp in slot_copies(s + RING, b):
                cp.start()

        return carry

    lax.fori_loop(0, slots, slot_step, 0)

    def ret_copy(i):
        d, f = plan.blocks[i]
        j = plan.neg[i]
        return pltpu.make_async_remote_copy(
            src_ref=ret.at[pl.ds(plan.off[i], plan.cap[i])], dst_ref=back.at[pl.ds(plan.off[j], plan.cap[j])],
            send_sem=ret_s.at[i], recv_sem=ret_r.at[j], device_id=peer(d, f), device_id_type=MESH)

    for g in range(plan.groups - 1, -1, -1):
        mg = plan.grp_rows[g]
        rows_g = slots * mg
        lo = [sum(plan.quota[4 * g:4 * g + i4]) for i4 in range(5)]

        def source(v):
            _, w = divmod_const(v, mg)
            src = jnp.zeros(v.shape, jnp.int32)
            for i4 in range(1, 4):
                src = jnp.where(w >= lo[i4], i4, src)
            return src

        r_row, r_col = iota((1, rows_g), 1), iota((rows_g, 1), 0)
        s_row, s_col = source(r_row), source(r_col)
        prefix = onehot((s_col == s_row) & (r_col < r_row))
        used = sels[g]
        p_row = dot(used.astype(BF16), prefix)[0:1]
        used_row = used[0:1]
        c0 = plan.off[4 * g]
        cg = sum(plan.cap[4 * g:4 * g + 4])
        q_col = iota((cg, 1), 0)
        src_q = jnp.zeros((cg, 1), jnp.int32)
        base_q = jnp.zeros((cg, 1), jnp.int32)
        for i4 in range(1, 4):
            o = plan.off[4 * g + i4] - c0
            src_q = jnp.where(q_col >= o, i4, src_q)
            base_q = jnp.where(q_col >= o, o, base_q)
        pick = onehot((p_row.astype(jnp.int32) == q_col - base_q) & (src_q == s_row) & (used_row > 0.5))
        o_g = xo[:, plan.grp_off[g]:plan.grp_off[g] + mg, :].reshape(rows_g, dim)
        out = dot(pick, o_g).astype(BF16)
        ret[c0:c0 + cg, :] = out
        if g == 0:
            back[0:plan.cap[0], :] = out[0:plan.cap[0]]
        for i in range(4 * g, 4 * g + 4):
            if i > 0:
                ret_copy(i).start()

    q_iota = iota((1, plan.rows), 1)
    take = onehot(q_c == q_iota)

    for cp in sends:
        cp.wait_send()
    for i in range(1, n):
        meta_copy(i).wait_send()
    for g in range(1, n_dp):
        flag_copy(g).wait()
    flag = flags[0]
    for g in range(1, n_dp):
        flag = jnp.maximum(flag, flags[g])
    flag_ref[...] = flag

    for i in range(1, n):
        ret_copy(plan.neg[i]).wait_recv()
    step = 256
    for j in range(0, dim, step):
        got = dot(take, back[:, j:j + step])
        acc = z_ref[:, j:j + step]
        tot = weight[0] * got[0:tok]
        for k in range(1, top_k):
            tot = tot + weight[k] * got[k * tok:(k + 1) * tok]
        y_ref[:, j:j + step] = (acc + tot).astype(BF16)
    for i in range(1, n):
        ret_copy(i).wait_send()


def fast_step(n, n_dp, x, slot_expert, w1, w3, w2, assign, w_router, s1, s3, s2):
    tok, dim = x.shape
    slots, _, ff = w1.shape
    plan = Plan(n, tok, assign.shape[1], slots)
    num = slots * n
    sp = -(-num // 128) * 128
    se = jnp.pad(slot_expert, (0, sp - num), constant_values=-2)
    vmem = pl.BlockSpec(memory_space=pltpu.VMEM)
    anym = pl.BlockSpec(memory_space=pl.ANY)
    dma, sh = pltpu.SemaphoreType.DMA, (plan.nz, 2)
    return pl.pallas_call(
        functools.partial(step_kernel, plan, n_dp),
        out_shape=(jax.ShapeDtypeStruct((tok, dim), BF16), jax.ShapeDtypeStruct((8, 128), F32)),
        in_specs=[vmem] * 5 + [anym] * 6,
        out_specs=(vmem, vmem),
        scratch_shapes=[
            pltpu.VMEM((n, tok, dim), BF16),
            pltpu.VMEM((slots, plan.m, dim), BF16),
            pltpu.VMEM((plan.rows, dim), BF16),
            pltpu.VMEM((plan.rows, dim), BF16),
            pltpu.VMEM((tok, dim), F32),
            pltpu.VMEM((8, 128), F32),
            pltpu.VMEM((n, 8, 128), F32),
            pltpu.VMEM((n_dp, 8, 128), F32),
            pltpu.VMEM((RING, dim, ff), BF16),
            pltpu.VMEM((RING, dim, ff), BF16),
            pltpu.VMEM((RING, ff, dim), BF16),
            dma((RING, 3)), dma(sh), dma(sh), dma(sh), dma(sh), dma((n,)), dma((n,)), dma((n_dp,)), dma((n_dp,)), dma((n,)), dma((n,)),
        ],
        compiler_params=pltpu.CompilerParams(collective_id=0, has_side_effects=True, vmem_limit_bytes=64 * 1024 * 1024 - 65536),
    )(x, assign, se.reshape(1, sp), se.reshape(sp, 1), w_router, w1, w3, w2, s1, s3, s2)


def solution(mesh):
    n, n_dp = mesh.shape['ep'], mesh.shape['dp']

    def device_step(*args):
        y, flag = fast_step(n, n_dp, *args)
        return lax.cond(jnp.max(flag) > 0.5, lambda: plain_step(n, *args), lambda: y)

    token_spec = P(('dp', 'ep'), None)
    slot_spec = P('ep', None, None)
    return jax.shard_map(device_step, mesh=mesh, in_specs=(token_spec, P(), slot_spec, slot_spec, slot_spec, token_spec, P(), P(), P(), P()), out_specs=token_spec, check_vma=False)
```

time: 282 us -> 96.2 us (0.34)
  blocking collectives: 101 us -> 0 us
  Pallas kernels: 0 us -> 86.9 us
  waiting for transfers between devices: 76.1 us -> 0 us
  matrix products: 53.5 us -> 0 us
  local copies, waits for them, and re-layouts: 37.5 us -> 6.89 us
  other arithmetic: 8.2 us -> 1.29 us
  starting transfers between devices: 4.98 us -> 0 us
    all_to_all x1 -> x0, blocking collectives: 101 us -> none  [device_step(): recv_rows = lax.all_to_all(send_rows, 'ep', 0, 0, tiled=True)]
    pallas_call x0 -> x1, Pallas kernels: none -> 86.9 us  [fast_step(): pl.pallas_call(functools.partial(step_kernel, plan, n_dp), out_shape=(jax...]
    all_to_all x1 -> x0, waiting for transfers between devices: 76.1 us -> none  [device_step(): lax.all_to_all(expert_out.reshape(dummy_row, dim_model), 'ep', 0, 0, tile...]
    dot_general x5 -> x0, matrix products: 53.5 us -> none  [the longest x1 27 us: device_step(): jnp.einsum('jlcf,lfd->jlcd', mid_act, w2_slots, preferred_element_type=jn...]
    gather x8 -> x0, local copies, waits for them, and re-layouts: 21.5 us -> none  [the longest x2 9.95 us: device_step(): jnp.take(back_rows, jnp.minimum(row_pos, dummy_row - 1), axis=0)]
    all_to_all x2 -> x0, local copies, waits for them, and re-layouts: 10.2 us -> none  [the longest x1 6.16 us: device_step(): lax.all_to_all(expert_out.reshape(dummy_row, dim_model), 'ep', 0, 0, tile...]
    all_to_all x1 -> x0, starting transfers between devices: 4.98 us -> none  [device_step(): lax.all_to_all(expert_out.reshape(dummy_row, dim_model), 'ep', 0, 0, tile...]
    reduce_sum x3 -> x0, other arithmetic: 3.98 us -> none  [the longest x1 3.63 us: device_step(): routed = jnp.sum(route_weight[:, :, None] * gathered, axis=1)]
  transfers between devices with their start and end apart: 1 -> 0, of which waited for: 1 -> 0; matrix products, arithmetic and copies ran while one was open for 4% -> 0% of each run, Pallas kernels for 0% -> 0%
where the time goes in v1:
time: 96.2 us; the launch traced here: 96 us
  Pallas kernels  86.9 us (90%)
  local copies, waits for them, and re-layouts  6.89 us (7%)
  other arithmetic  1.29 us (1%)
    pallas_call x1, Pallas kernels, fast_step(): pl.pallas_call(functools.partial(step_kernel, plan, n_dp), out_shape=(jax...  86.9 us
    unnamed x3, local copies, waits for them, and re-layouts  4.83 us

profile of v1, /device:TPU:21, one launch (start us, length us, event | category | flops | bytes accessed | tf_op | source)
XLA Modules:
  0.0 96.0 jit_solution(3002804006319504520)
XLA Ops:
  0.0 0.7 pad.4
  0.7 0.8 reshape.207.se_col_ref
  1.5 0.6 reshape.156.se_row_ref
  2.1 1.8 %copy.46.wr_ref = bf16[1536,64]{1,0:T(8,128)(2,1)} copy(bf16[1536,64]{0,1:T(8,128)(2,1)} %param.18) | data formatting | bytes 393216 | tf_op args[6]
  3.9 1.4 %copy.44.assign_ref = s32[64,6]{1,0:T(8,128)} copy(s32[64,6]{0,1:T(8,128)} %param.17) | data formatting | bytes 3072 | tf_op args[5]
  5.3 86.9 %shard_map.102 = (bf16[64,1536]{1,0:T(8,128)(2,1)}, f32[8,128]{1,0:T(8,128)}) custom-call(bf16[64,1536]{1,0:T(8,128)(2,1)} %x_ref.1, s32[64,6]{1,0:T(8,128)} %copy.44.assign_ref, s32[1,384]{1,0:T(1,128)} %reshape.156.se_row_ref, s32[384,1]{1,0:T(8,128)} %reshape.207.se_col_ref, bf16[1536,64]{1,0:T(8,128)(2,1)} %copy.46.wr_ref, ...), custom_call_target="tpu_custom_call" | custom-call | tf_op jit(solution)/shard_map/pallas_call | solution.py:478
  92.2 1.3 %reduce_max.9 = f32[]{:T(128)} reduce(f32[8,128]{1,0:T(8,128)} %get-tuple-element.41, f32[]{:T(128)} %constant.105.clone.1), dimensions={0,1}, to_apply=%region_0.1 | reduce | flops 1023 | bytes 4104 | tf_op jit(solution)/shard_map/reduce_max | solution.py:506
  94.1 0.2 conditional.1
  94.4 1.6 %copy.56 = bf16[64,1536]{1,0:T(8,128)(2,1)} copy(bf16[64,1536]{1,0:T(8,128)(2,1)} %get-tuple-element.43) | data formatting | bytes 393216
